TPU v7x, 32 devices: a whole 2x2x4 slice. The times are simulated.
32 devices in a mesh: section: 2 (over y), dp: 8 (over z, core), vocab: 2 (over x).
Axes of the slice: x: 2, y: 2, z: 4, core: 2. Of those that a mesh axis runs over, the one named last changes fastest.
Arguments:
- activations: bfloat16 [2, 1024, 2048], P('section', 'dp'), may hold values from -32 to 32
- token_ids: int32 [2, 1024], replicated, may hold values from 0 to 8191
- embed_table: bfloat16 [8192, 2048], P(('dp', 'vocab')), may hold values from -3 to 3
Outputs:
- tied_grad: bfloat16 [16, 2, 256, 2048], P(('dp', 'vocab'), 'section')
All inputs are finite; a program needn't handle non-finite values.
Results may differ from a plain program's by a relative error of at most 0.0029.
Values may be sent and summed in bfloat16 or wider, within the bound.
A program may use at most 128 MiB of HBM per device.

v0:
```python
import jax
import jax.numpy as jnp
from jax import lax
from jax.sharding import PartitionSpec as P


def from_partner(block, axis, apart):
    count = lax.axis_size(axis)
    route = []
    for low in range(count):
        high = low | 1 << apart
        if high != low and high < count:
            route += [(low, high), (high, low)]
    return lax.ppermute(block, axis, route)


def spread_rows(row_tuple):
    return (
        lax.all_gather(row_tuple[0], "dp", axis=0, tiled=True),
        lax.all_gather(row_tuple[1], "dp", axis=0, tiled=True),
    )


def local_stats(logits):
    row_peak = jnp.max(logits, axis=1)
    row_total = jnp.sum(jnp.exp(logits - row_peak[:, None]), axis=1)
    return (row_peak, row_total)


def body(activations, token_ids, embed_table):
    own_rows = activations[0]
    model_width = own_rows.shape[1]
    table_count = embed_table.shape[0]
    section_index = lax.axis_index("section")
    half_rows = table_count // lax.axis_size("section")
    block_first = (
        lax.axis_index("dp") * lax.axis_size("vocab") + lax.axis_index("vocab")
    ) * table_count
    partner = from_partner(own_rows, "section", 0)
    cot_rows = jnp.where(section_index == 0, own_rows, partner)
    hid_rows = jnp.where(section_index == 0, partner, own_rows)
    cot_all, hid_all = spread_rows((cot_rows, hid_rows))
    my_table = lax.dynamic_slice_in_dim(embed_table, section_index * half_rows, half_rows, 0)
    row_first = block_first + section_index * half_rows
    positions = jnp.arange(half_rows, dtype=jnp.int32)[None, :]
    target_hot = (token_ids[1] - row_first)[:, None] == positions
    input_hot = (token_ids[0] - row_first)[:, None] == positions
    logits = lax.dot_general(
        hid_all, my_table, (((1,), (1,)), ((), ())), preferred_element_type=jnp.float32
    )
    row_peak, row_total = local_stats(logits)
    peak_all = lax.pmax(row_peak, ("section", "dp", "vocab"))
    total_all = lax.psum(row_total * jnp.exp(row_peak - peak_all), ("section", "dp", "vocab"))
    probs = jnp.exp(logits - peak_all[:, None]) / total_all[:, None]
    last_part = (probs - target_hot.astype(jnp.float32)).astype(jnp.bfloat16)
    first_part = input_hot.astype(jnp.bfloat16)
    summed = lax.dot_general(
        last_part, hid_all, (((0,), (0,)), ((), ())), preferred_element_type=jnp.float32
    )
    summed = summed + lax.dot_general(
        first_part, cot_all, (((0,), (0,)), ((), ())), preferred_element_type=jnp.float32
    )
    return summed.astype(jnp.bfloat16).reshape(1, 1, half_rows, model_width)


def solution(mesh):
    return jax.shard_map(
        body,
        mesh=mesh,
        in_specs=(P("section", "dp", None), P(), P(("dp", "vocab"), None)),
        out_specs=P(("dp", "vocab"), "section", None, None),
        check_vma=False,
    )
```

profile of v0, /device:TPU:0, one launch (start us, length us, event | category | flops | bytes accessed | tf_op | source)
XLA Modules:
  0.0 170.4 jit_solution(3358210218269821049)
XLA Ops:
  6.5 0.0 copy-start
  6.5 0.0 all-gather.3.cloned.1.call-start
  6.5 3.0 %collective-permute-start = (bf16[128,2048]{1,0:T(8,128)(2,1)}, bf16[128,2048]{1,0:T(8,128)(2,1)S(1)}, u32[]{:S(2)}, u32[]{:S(2)}) collective-permute-start(bf16[128,2048]{1,0:T(8,128)(2,1)} %bitcast.10), channel_id=1, source_target_pairs={{0,16},{16,0},{1,17},{17,1},{2,18},{18,2},{3,19},{19,3},{4,20},{20... | collective-permute-start | bytes 1572872 | tf_op jit(solution)/shard_map/ppermute | solution.py:14
  9.5 12.1 %collective-permute-done = bf16[128,2048]{1,0:T(8,128)(2,1)S(1)} collective-permute-done((bf16[128,2048]{1,0:T(8,128)(2,1)}, bf16[128,2048]{1,0:T(8,128)(2,1)S(1)}, u32[]{:S(2)}, u32[]{:S(2)}) %collective-permute-start) | collective-permute-done | bytes 524320 | tf_op jit(solution)/shard_map/ppermute | solution.py:14
  21.7 2.1 %broadcast_select_fusion.1 = (bf16[128,2048]{1,0:T(8,128)(2,1)}, bf16[128,2048]{1,0:T(8,128)(2,1)}) fusion(bf16[128,2048]{1,0:T(8,128)(2,1)S(1)} %collective-permute-done, pred[]{:T(512)S(6)} %eq.14, bf16[1,128,2048]{2,1,0:T(8,128)(2,1)} %param.3), kind=kLoop, calls=%fused_computation.15 | loop fusion | flops 524288 | bytes 2097153 | tf_op jit(solution)/shard_map/jit(_where)/select_n | solution.py:41
  23.8 0.0 all-gather.3.cloned.1.call-update
  23.8 0.0 all-gather.5.cloned.1.call-start
  23.9 0.7 all-gather.5.cloned.1.call-update
  24.6 0.8 slice_subtract_fusion.1
  25.4 46.9 %all-gather.3.cloned.1.call-done = bf16[1024,2048]{1,0:T(8,128)(2,1)} async-done(((bf16[128,2048]{1,0:T(8,128)(2,1)}), bf16[1024,2048]{1,0:T(8,128)(2,1)}) %all-gather.3.cloned.1.call-update) | async-done | bytes 4194320 | tf_op jit(solution)/shard_map/all_gather | solution.py:20
  72.3 0.0 copy-done
  72.3 3.5 %fusion.10 = (f32[1024]{0:T(1024)S(1)}, f32[1024,256]{0,1:T(8,128)S(1)}) fusion(bf16[1024,2048]{1,0:T(8,128)(2,1)} %all-gather.3.cloned.1.call-done, bf16[512,2048]{1,0:T(8,128)(2,1)S(1)} %copy-done, s32[]{:T(128)S(6)} %select_n.17), kind=kOutput, calls=%fused_computation.20 | convolution fusion | flops 1074002944 | bytes 6295556 | tf_op jit(solution)/shard_map/dot_general | solution.py:48
  75.8 42.2 %pmax.7 = f32[1024]{0:T(1024)S(1)} all-reduce(f32[1024]{0:T(1024)S(1)} %get-tuple-element.9), channel_id=1, replica_groups=mesh['section'=2,'dp'=8,'vocab'=2] {'section','dp','vocab'}, use_global_device_ids=true, to_apply=%region_1.2 | all-reduce | flops 1024 | bytes 8192 | tf_op jit(solution)/shard_map/pmax | solution.py:52
  118.0 0.2 exponential_reduce_fusion
  118.2 39.3 %psum.7 = f32[1024]{0:T(1024)S(1)} all-reduce(f32[1024]{0:T(1024)S(1)} %exponential_multiply_fusion), channel_id=1, replica_groups=mesh['section'=2,'dp'=8,'vocab'=2] {'section','dp','vocab'}, use_global_device_ids=true, to_apply=%region_3.4 | all-reduce | flops 1024 | bytes 8192 | tf_op jit(solution)/shard_map/psum | solution.py:53
  157.5 0.0 all-gather.5.cloned.1.call-done
  157.5 0.0 copy-start.1
  157.5 3.7 %fusion.4 = f32[256,2048]{1,0:T(8,128)S(1)} fusion(bf16[1024,2048]{1,0:T(8,128)(2,1)} %all-gather.5.cloned.1.call-done, s32[1024]{0:T(1024)S(1)} %bitcast.12), kind=kOutput, calls=%fused_computation.9 | convolution fusion | flops 1074003968 | bytes 6295552 | tf_op jit(solution)/shard_map/dot_general | solution.py:60
  161.2 0.0 copy-done.1
  161.2 2.3 %fusion.1 = bf16[1,1,256,2048]{3,2,1,0:T(8,128)(2,1)} fusion(f32[256,2048]{1,0:T(8,128)S(1)} %fusion.4, bf16[1024,2048]{1,0:T(8,128)(2,1)S(1)} %copy-done.1, f32[1024,256]{0,1:T(8,128)S(1)} %get-tuple-element.10, s32[1024]{0:T(1024)S(1)} %bitcast.11, f32[1024]{0:T(1024)S(1)} %psum.7, f32[1024]{0:T(1024)S(1)} %pmax.7), kind=kOutput, calls=%fused_computation.2 | convolution fusion | flops 1076363264 | bytes 8400896 | tf_op jit(solution)/shard_map/dot_general | solution.py:57
  (1 shorter events, 0.0 us)
Async XLA Ops:
  6.5 65.8 %copy-start = (bf16[512,2048]{1,0:T(8,128)(2,1)S(1)}, bf16[512,2048]{1,0:T(8,128)(2,1)}, u32[]{:S(2)}) copy-start(bf16[512,2048]{1,0:T(8,128)(2,1)} %param.5) | copy-start | bytes 6291460
  6.5 65.8 %all-gather.3.cloned.1.call-start = ((), (), s32[]{:S(2)}) async-start(), calls=%async_computation | async-start | bytes 4718592 | tf_op jit(solution)/shard_map/all_gather | solution.py:20
  6.5 15.1 %collective-permute-start = (bf16[128,2048]{1,0:T(8,128)(2,1)}, bf16[128,2048]{1,0:T(8,128)(2,1)S(1)}, u32[]{:S(2)}, u32[]{:S(2)}) collective-permute-start(bf16[128,2048]{1,0:T(8,128)(2,1)} %bitcast.10), channel_id=1, source_target_pairs={{0,16},{16,0},{1,17},{17,1},{2,18},{18,2},{3,19},{19,3},{4,20},{20... | collective-permute-start | bytes 1572872 | tf_op jit(solution)/shard_map/ppermute | solution.py:14
  23.8 133.7 %all-gather.5.cloned.1.call-start = ((), (), s32[]{:S(2)}) async-start(), calls=%async_computation.1 | async-start | bytes 4718592 | tf_op jit(solution)/shard_map/all_gather | solution.py:19
  157.5 3.7 %copy-start.1 = (bf16[1024,2048]{1,0:T(8,128)(2,1)S(1)}, bf16[1024,2048]{1,0:T(8,128)(2,1)}, u32[]{:S(2)}) copy-start(bf16[1024,2048]{1,0:T(8,128)(2,1)} %all-gather.3.cloned.1.call-done) | copy-start | bytes 12582916
Sparse Core Ops, SparseCore 0:
  23.9 48.3 all-gather.2
  73.9 46.7 all-gather.4
where the time goes:
time: 171 us; the launch traced here: 170 us
  blocking collectives  81.5 us (48%)
  waiting for transfers between devices  59.8 us (35%)
  between operations  13.4 us (8%)
  matrix products  9.52 us (6%)
  other arithmetic  3.09 us (2%)
  starting transfers between devices  3.04 us (2%)
    all_gather x1, waiting for transfers between devices, spread_rows(): lax.all_gather(row_tuple[1], 'dp', axis=0, tiled=True)  46.9 us
    pmax x1, blocking collectives, body(): peak_all = lax.pmax(row_peak, ('section', 'dp', 'vocab'))  42.2 us
    psum x1, blocking collectives, body(): lax.psum(row_total * jnp.exp(row_peak - peak_all), ('section', 'dp', 'voc...  39.3 us
    ppermute x1, waiting for transfers between devices, from_partner(): return lax.ppermute(block, axis, route)  12.1 us
    dot_general x1, matrix products, body(): lax.dot_general(first_part, cot_all, (((0,), (0,)), ((), ())), preferred_...  3.7 us
    dot_general x1, matrix products, body(): lax.dot_general(hid_all, my_table, (((1,), (1,)), ((), ())), preferred_el...  3.48 us
  transfers between devices with their start and end apart: 3, of which 2 were waited for; matrix products, arithmetic and copies ran while one was open for 3% of the time, Pallas kernels for 0%

commit v1 on v0

--- a/solution.py
+++ b/solution.py
@@ -50,7 +50,9 @@
     )
     row_peak, row_total = local_stats(logits)
     peak_all = lax.pmax(row_peak, ("section", "dp", "vocab"))
-    total_all = lax.psum(row_total * jnp.exp(row_peak - peak_all), ("section", "dp", "vocab"))
+    total_all = row_total * jnp.exp(row_peak - peak_all)
+    for mesh_axis in (("dp", "vocab"), "section"):
+        total_all = lax.psum(total_all, mesh_axis)
     probs = jnp.exp(logits - peak_all[:, None]) / total_all[:, None]
     last_part = (probs - target_hot.astype(jnp.float32)).astype(jnp.bfloat16)
     first_part = input_hot.astype(jnp.bfloat16)

time: 171 us -> 168 us (0.982)
  blocking collectives: 81.5 us -> 78.9 us
    psum x1 -> x2, blocking collectives: 39.3 us -> 36.7 us  [body(): total_all = lax.psum(total_all, mesh_axis)]
where the time goes in v1:
time: 168 us
  blocking collectives  78.9 us (47%)
  waiting for transfers between devices  59.8 us (36%)
  between operations  13.4 us (8%)
  matrix products  9.51 us (6%)
  other arithmetic  3.1 us (2%)
  starting transfers between devices  3.04 us (2%)
    all_gather x1, waiting for transfers between devices, spread_rows(): lax.all_gather(row_tuple[1], 'dp', axis=0, tiled=True)  46.9 us
    pmax x1, blocking collectives, body(): peak_all = lax.pmax(row_peak, ('section', 'dp', 'vocab'))  42.2 us
    psum x2, blocking collectives, body(): total_all = lax.psum(total_all, mesh_axis)  36.7 us
    ppermute x1, waiting for transfers between devices, from_partner(): return lax.ppermute(block, axis, route)  12.1 us
    dot_general x1, matrix products, body(): lax.dot_general(first_part, cot_all, (((0,), (0,)), ((), ())), preferred_...  3.7 us
    dot_general x1, matrix products, body(): lax.dot_general(hid_all, my_table, (((1,), (1,)), ((), ())), preferred_el...  3.47 us
  transfers between devices with their start and end apart: 3, of which 2 were waited for; matrix products, arithmetic and copies ran while one was open for 3% of the time, Pallas kernels for 0%

profile of v1, /device:TPU:0, one launch (start us, length us, event | category | flops | bytes accessed | tf_op | source)
XLA Modules:
  0.0 167.8 jit_solution(1250322285658928466)
XLA Ops:
  6.5 0.0 copy-start
  6.5 0.0 all-gather.3.cloned.1.call-start
  6.5 3.0 %collective-permute-start = (bf16[128,2048]{1,0:T(8,128)(2,1)}, bf16[128,2048]{1,0:T(8,128)(2,1)S(1)}, u32[]{:S(2)}, u32[]{:S(2)}) collective-permute-start(bf16[128,2048]{1,0:T(8,128)(2,1)} %bitcast.10), channel_id=1, source_target_pairs={{0,16},{16,0},{1,17},{17,1},{2,18},{18,2},{3,19},{19,3},{4,20},{20... | collective-permute-start | bytes 1572872 | tf_op jit(solution)/shard_map/ppermute | solution.py:14
  9.5 12.1 %collective-permute-done = bf16[128,2048]{1,0:T(8,128)(2,1)S(1)} collective-permute-done((bf16[128,2048]{1,0:T(8,128)(2,1)}, bf16[128,2048]{1,0:T(8,128)(2,1)S(1)}, u32[]{:S(2)}, u32[]{:S(2)}) %collective-permute-start) | collective-permute-done | bytes 524320 | tf_op jit(solution)/shard_map/ppermute | solution.py:14
  21.7 2.1 %broadcast_select_fusion.1 = (bf16[128,2048]{1,0:T(8,128)(2,1)}, bf16[128,2048]{1,0:T(8,128)(2,1)}) fusion(bf16[128,2048]{1,0:T(8,128)(2,1)S(1)} %collective-permute-done, pred[]{:T(512)S(6)} %eq.14, bf16[1,128,2048]{2,1,0:T(8,128)(2,1)} %param.3), kind=kLoop, calls=%fused_computation.15 | loop fusion | flops 524288 | bytes 2097153 | tf_op jit(solution)/shard_map/jit(_where)/select_n | solution.py:41
  23.8 0.0 all-gather.3.cloned.1.call-update
  23.8 0.0 all-gather.5.cloned.1.call-start
  23.9 0.7 all-gather.5.cloned.1.call-update
  24.6 0.8 slice_subtract_fusion.1
  25.4 46.9 %all-gather.3.cloned.1.call-done = bf16[1024,2048]{1,0:T(8,128)(2,1)} async-done(((bf16[128,2048]{1,0:T(8,128)(2,1)}), bf16[1024,2048]{1,0:T(8,128)(2,1)}) %all-gather.3.cloned.1.call-update) | async-done | bytes 4194320 | tf_op jit(solution)/shard_map/all_gather | solution.py:20
  72.3 0.0 copy-done
  72.3 3.5 %fusion.10 = (f32[1024]{0:T(1024)S(1)}, f32[1024,256]{0,1:T(8,128)S(1)}) fusion(bf16[1024,2048]{1,0:T(8,128)(2,1)} %all-gather.3.cloned.1.call-done, bf16[512,2048]{1,0:T(8,128)(2,1)S(1)} %copy-done, s32[]{:T(128)S(6)} %select_n.17), kind=kOutput, calls=%fused_computation.20 | convolution fusion | flops 1074002944 | bytes 6295556 | tf_op jit(solution)/shard_map/dot_general | solution.py:48
  75.8 42.2 %pmax.7 = f32[1024]{0:T(1024)S(1)} all-reduce(f32[1024]{0:T(1024)S(1)} %get-tuple-element.9), channel_id=1, replica_groups=mesh['section'=2,'dp'=8,'vocab'=2] {'section','dp','vocab'}, use_global_device_ids=true, to_apply=%region_1.2 | all-reduce | flops 1024 | bytes 8192 | tf_op jit(solution)/shard_map/pmax | solution.py:52
  118.0 0.2 exponential_reduce_fusion
  118.2 31.8 %psum.14 = f32[1024]{0:T(1024)S(1)} all-reduce(f32[1024]{0:T(1024)S(1)} %exponential_multiply_fusion), channel_id=1, replica_groups=mesh['section'=2,'dp'=8,'vocab'=2] {'dp','vocab'}, use_global_device_ids=true, to_apply=%region_3.4 | all-reduce | flops 1024 | bytes 8192 | tf_op jit(solution)/shard_map/psum | solution.py:55
  150.0 4.9 %psum.15 = f32[1024]{0:T(1024)S(1)} all-reduce(f32[1024]{0:T(1024)S(1)} %psum.14), channel_id=1, replica_groups=mesh['section'=2,'dp'=8,'vocab'=2] {'section'}, use_global_device_ids=true, to_apply=%region_4.5 | all-reduce | flops 1024 | bytes 8192 | tf_op jit(solution)/shard_map/psum | solution.py:55
  154.9 0.0 all-gather.5.cloned.1.call-done
  154.9 0.0 copy-start.1
  154.9 3.7 %fusion.4 = f32[256,2048]{1,0:T(8,128)S(1)} fusion(bf16[1024,2048]{1,0:T(8,128)(2,1)} %all-gather.5.cloned.1.call-done, s32[1024]{0:T(1024)S(1)} %bitcast.12), kind=kOutput, calls=%fused_computation.9 | convolution fusion | flops 1074003968 | bytes 6295552 | tf_op jit(solution)/shard_map/dot_general | solution.py:62
  158.6 0.0 copy-done.1
  158.6 2.3 %fusion.1 = bf16[1,1,256,2048]{3,2,1,0:T(8,128)(2,1)} fusion(f32[256,2048]{1,0:T(8,128)S(1)} %fusion.4, bf16[1024,2048]{1,0:T(8,128)(2,1)S(1)} %copy-done.1, f32[1024,256]{0,1:T(8,128)S(1)} %get-tuple-element.10, s32[1024]{0:T(1024)S(1)} %bitcast.11, f32[1024]{0:T(1024)S(1)} %psum.15, f32[1024]{0:T(1024)S(1)} %pmax.7), kind=kOutput, calls=%fused_computation.2 | convolution fusion | flops 1076363264 | bytes 8400896 | tf_op jit(solution)/shard_map/dot_general | solution.py:59
  (1 shorter events, 0.0 us)
Async XLA Ops:
  6.5 65.8 %copy-start = (bf16[512,2048]{1,0:T(8,128)(2,1)S(1)}, bf16[512,2048]{1,0:T(8,128)(2,1)}, u32[]{:S(2)}) copy-start(bf16[512,2048]{1,0:T(8,128)(2,1)} %param.5) | copy-start | bytes 6291460
  6.5 65.8 %all-gather.3.cloned.1.call-start = ((), (), s32[]{:S(2)}) async-start(), calls=%async_computation | async-start | bytes 4718592 | tf_op jit(solution)/shard_map/all_gather | solution.py:20
  6.5 15.1 %collective-permute-start = (bf16[128,2048]{1,0:T(8,128)(2,1)}, bf16[128,2048]{1,0:T(8,128)(2,1)S(1)}, u32[]{:S(2)}, u32[]{:S(2)}) collective-permute-start(bf16[128,2048]{1,0:T(8,128)(2,1)} %bitcast.10), channel_id=1, source_target_pairs={{0,16},{16,0},{1,17},{17,1},{2,18},{18,2},{3,19},{19,3},{4,20},{20... | collective-permute-start | bytes 1572872 | tf_op jit(solution)/shard_map/ppermute | solution.py:14
  23.8 131.1 %all-gather.5.cloned.1.call-start = ((), (), s32[]{:S(2)}) async-start(), calls=%async_computation.1 | async-start | bytes 4718592 | tf_op jit(solution)/shard_map/all_gather | solution.py:19
  154.9 3.7 %copy-start.1 = (bf16[1024,2048]{1,0:T(8,128)(2,1)S(1)}, bf16[1024,2048]{1,0:T(8,128)(2,1)}, u32[]{:S(2)}) copy-start(bf16[1024,2048]{1,0:T(8,128)(2,1)} %all-gather.3.cloned.1.call-done) | copy-start | bytes 12582916
Sparse Core Ops, SparseCore 0:
  23.9 48.3 all-gather.2
  73.9 46.7 all-gather.4
